TPU v7x, 512 devices: a whole 4x4x16 slice. The times are simulated.
512 devices in a mesh: tm: 16 (over y_lo, x, core), rep: 32 (over y_hi, z).
Axes of the slice: x: 4, y: 4 (y_hi: 2, y_lo: 2; y = y_hi * 2 + y_lo), z: 16, core: 2. Of those that a mesh axis runs over, the one named last changes fastest.
Arguments:
- snapshots: float32 [128, 256, 1024], P('tm', 'rep'), may hold values from -6 to 6
- freq_bins: int32 [32], replicated, may hold values from 1 to 511
- replicas: float32 [2, 32, 32768, 256], P(None, 'tm', 'rep'), may hold values from -6 to 6
Outputs:
- power: float32 [32768], P(('rep', 'tm'))
All inputs are finite; a program needn't handle non-finite values.
Results may differ from a plain program's by a relative error of at most 0.00005.
Values sent between devices are 32-bit elements; how exact they have to be, the bound alone decides.
A program may use at most 64 MiB of HBM per device.

v0:
```python
import math

import jax
import jax.numpy as jnp
from jax import lax
from jax.sharding import PartitionSpec as P

epsilon = 1e-06


def dft_table(freq_bins, length):
    offsets = jnp.arange(length, dtype=jnp.int32)
    phases = offsets[:, None] * freq_bins[None, :] % length
    angles = phases.astype(jnp.float32) * (2.0 * math.pi / length)
    window = 0.5 - 0.5 * jnp.cos(offsets.astype(jnp.float32) * (2.0 * math.pi / length))
    return jnp.concatenate(
        [window[:, None] * jnp.cos(angles), -window[:, None] * jnp.sin(angles)], axis=1
    )


def matmul(left, right):
    return jnp.dot(left, right, precision=lax.Precision.HIGHEST, preferred_element_type=jnp.float32)


def shards(snapshots, freq_bins, replicas):
    snap_rows, elem_rows, samples = snapshots.shape
    bin_count = freq_bins.shape[0]
    dft_rows = dft_table(freq_bins, samples)
    spectra = matmul(snapshots.reshape(snap_rows * elem_rows, samples), dft_rows).reshape(
        snap_rows, elem_rows, 2, bin_count
    )
    gathered = lax.all_gather(spectra, "rep", axis=1, tiled=True)
    by_owner = lax.all_to_all(gathered, "tm", split_axis=3, concat_axis=0, tiled=True)
    total_snaps = by_owner.shape[0]
    elem_count = by_owner.shape[1]
    local_bins = by_owner.shape[3]
    running = jnp.zeros((replicas.shape[2],), jnp.float32)
    for column in range(local_bins):
        spec_re = by_owner[:, :, 0, column]
        spec_im = by_owner[:, :, 1, column]
        rep_re = replicas[0, column]
        rep_im = replicas[1, column]
        power_trace = jnp.sum(spec_re * spec_re + spec_im * spec_im) / total_snaps + epsilon
        norm_sq = jnp.sum(rep_re * rep_re + rep_im * rep_im, axis=1) + epsilon
        csd_re = (matmul(spec_re.T, spec_re) + matmul(spec_im.T, spec_im)) / total_snaps
        csd_im = (matmul(spec_im.T, spec_re) - matmul(spec_re.T, spec_im)) / total_snaps
        applied_re = matmul(rep_re, csd_re.T) - matmul(rep_im, csd_im.T)
        applied_im = matmul(rep_im, csd_re.T) + matmul(rep_re, csd_im.T)
        quadratic = jnp.sum(rep_re * applied_re + rep_im * applied_im, axis=1)
        running = running + quadratic / (norm_sq * power_trace / elem_count)
    partial_value = running / bin_count
    return lax.psum_scatter(partial_value, "tm", scatter_dimension=0, tiled=True)


def solution(mesh):
    in_specs = (P("tm", "rep", None), P(), P(None, "tm", "rep", None))
    out_specs = P(("rep", "tm"))
    return jax.shard_map(shards, mesh=mesh, in_specs=in_specs, out_specs=out_specs, check_vma=False)
```

profile of v0, /device:TPU:1, one launch (start us, length us, event | category | flops | bytes accessed | tf_op | source)
XLA Modules:
  0.0 168.3 jit_solution(13717904278462664921)
XLA Ops:
  0.0 0.0 copy-start
  0.0 1.3 cosine_multiply_fusion
  1.3 0.0 copy-done
  1.4 0.4 convolution_bitcast_fusion
  1.7 0.1 copy.32
  1.8 0.1 reshape.20
  1.9 82.0 %all_gather.3 = f32[8,256,2,32]{3,2,1,0:T(2,128)S(1)} all-gather(f32[8,8,2,32]{3,2,1,0:T(2,128)S(1)} %reshape.20), channel_id=1, replica_groups=mesh['tm'=16,'rep'=32] {'rep'}, dimensions={1}, use_global_device_ids=true | all-gather | bytes 540672 | tf_op jit(solution)/shard_map/all_gather | solution.py:32
  83.9 1.5 copy.33
  85.4 18.8 %all-to-all-start = ((f32[8,256,2,32]{1,0,2,3:T(8,128)}), f32[8,256,2,32]{1,0,2,3:T(8,128)}, u32[]{:S(2)}, u32[]{:S(2)}) async-start(f32[8,256,2,32]{1,0,2,3:T(8,128)} %copy.33), calls=%async_computation | async-start | bytes 1048576 | tf_op jit(solution)/shard_map/all_to_all | solution.py:33
  104.2 3.6 %fusion.56 = (f32[1,1,1024,256]{3,2,1,0:T(8,128)S(1)}, f32[1,1,1024,256]{3,2,1,0:T(8,128)S(1)}, f32[1,1,1024,256]{3,2,1,0:T(8,128)}, f32[1,1,1024,256]{3,2,1,0:T(8,128)S(1)}) fusion(f32[2,2,1024,256]{3,2,1,0:T(8,128)} %param.5), kind=kLoop, calls=%fused_computation.83 | loop fusion | bytes 8388608 | tf_op jit(solution)/shard_map/slice | solution.py:42
  107.8 1.3 copy.42
  109.1 0.3 copy.43
  109.5 0.3 copy.41
  109.8 1.6 copy.40
  111.4 1.3 dynamic-slice
  113.3 1.7 %fusion.29 = (f32[1024]{0:T(1024)S(1)}, f32[1024]{0:T(1024)S(1)}) fusion(f32[1,1,1024,256]{2,3,1,0:T(8,128)S(1)} %copy.43, f32[1,1,1024,256]{2,3,1,0:T(8,128)} %copy.42, f32[1,1,1024,256]{2,3,1,0:T(8,128)S(1)} %copy.41, f32[1,1,1024,256]{2,3,1,0:T(8,128)S(1)} %copy.40), kind=kLoop, calls=%fused_computation.39 | loop fusion | flops 2095104 | bytes 4202496 | tf_op jit(solution)/shard_map/reduce_sum | solution.py:44
  115.0 0.0 all-to-all-done
  115.0 0.0 copy-start.1
  115.0 1.2 copy.45
  116.3 0.4 fusion.45
  116.7 0.4 fusion.44
  117.1 0.4 fusion.13
  117.5 3.3 %fusion.20 = f32[256,1024]{1,0:T(8,128)} fusion(f32[256,256]{1,0:T(8,128)S(1)} %fusion.13, f32[2,2,1024,256]{3,2,1,0:T(8,128)} %param.5), kind=kOutput, calls=%fused_computation.29 | convolution fusion | flops 805306368 | bytes 2359296 | tf_op jit(solution)/shard_map/dot_general | solution.py:22
  120.8 0.0 copy-done.1
  120.8 2.0 %fusion.16 = f32[256,1024]{1,0:T(8,128)} fusion(f32[256,256]{1,0:T(8,128)S(1)} %fusion.13, f32[2,2,1024,256]{3,2,1,0:T(8,128)S(1)} %copy-done.1), kind=kOutput, calls=%fused_computation.25 | convolution fusion | flops 805306368 | bytes 2359296 | tf_op jit(solution)/shard_map/dot_general | solution.py:22
  122.8 0.4 fusion.43
  123.2 0.4 fusion.42
  123.7 0.4 fusion.15
  124.1 2.0 %fusion.26 = f32[256,1024]{1,0:T(8,128)} fusion(f32[256,256]{1,0:T(8,128)S(1)} %fusion.15, f32[2,2,1024,256]{3,2,1,0:T(8,128)S(1)} %copy-done.1), kind=kOutput, calls=%fused_computation.35 | convolution fusion | flops 805306368 | bytes 2359296 | tf_op jit(solution)/shard_map/dot_general | solution.py:22
  126.1 2.1 %fusion.22 = f32[256,1024]{1,0:T(8,128)} fusion(f32[256,256]{1,0:T(8,128)S(1)} %fusion.15, f32[2,2,1024,256]{3,2,1,0:T(8,128)S(1)} %copy-done.1), kind=kOutput, calls=%fused_computation.31 | convolution fusion | flops 805306368 | bytes 2359296 | tf_op jit(solution)/shard_map/dot_general | solution.py:22
  128.2 0.7 add_reduce_fusion.1
  128.9 1.1 fusion.12
  130.1 1.1 fusion.14
  132.5 0.0 copy-start.2
  132.6 0.0 copy-start.4
  132.6 0.0 copy-start.5
  132.6 3.2 %fusion.4 = f32[1024,256]{0,1:T(8,128)S(1)} fusion(f32[256,1024]{1,0:T(8,128)} %fusion.20, f32[256,256]{1,0:T(8,128)} %fusion.12, f32[1,1,1024,256]{2,3,1,0:T(8,128)} %copy.42, f32[2,2,1024,256]{3,2,1,0:T(8,128)} %param.5), kind=kOutput, calls=%fused_computation.6 | convolution fusion | flops 805830656 | bytes 4456448 | tf_op jit(solution)/shard_map/dot_general | solution.py:22
  135.8 0.0 copy-done.2
  135.8 0.0 copy-start.3
  135.8 2.6 %fusion.11 = f32[1024]{0:T(1024)S(1)} fusion(f32[1024,256]{0,1:T(8,128)S(1)} %fusion.4, f32[256,1024]{1,0:T(8,128)} %fusion.16, f32[256,256]{1,0:T(8,128)} %fusion.12, f32[1,1,1024,256]{2,3,1,0:T(8,128)S(1)} %copy.43, f32[2,2,1024,256]{3,2,1,0:T(8,128)S(1)} %copy-done.2), kind=kOutput, calls=%fused_computation.15 | convolution fusion | flops 806353920 | bytes 4460544 | tf_op jit(solution)/shard_map/dot_general | solution.py:22
  138.4 0.0 copy-done.4
  138.4 0.0 copy-done.5
  138.4 1.1 fusion.9
  139.5 0.0 copy-done.3
  139.5 1.2 fusion.10
  140.8 26.9 %all-reduce = f32[1024]{0:T(1024)S(1)} all-reduce(f32[1024]{0:T(1024)S(1)} %add_multiply_fusion), channel_id=2, replica_groups=mesh['tm'=16,'rep'=32] {'tm'}, use_global_device_ids=true, to_apply=%region_6.7.clone | all-reduce | flops 1024 | bytes 8192
  167.7 0.6 dynamic-slice.1
  (2 shorter events, 0.1 us)
Async XLA Ops:
  0.0 1.3 copy-start
  85.4 29.6 %all-to-all-start = ((f32[8,256,2,32]{1,0,2,3:T(8,128)}), f32[8,256,2,32]{1,0,2,3:T(8,128)}, u32[]{:S(2)}, u32[]{:S(2)}) async-start(f32[8,256,2,32]{1,0,2,3:T(8,128)} %copy.33), calls=%async_computation | async-start | bytes 1048576 | tf_op jit(solution)/shard_map/all_to_all | solution.py:33
  115.0 5.8 %copy-start.1 = (f32[2,2,1024,256]{3,2,1,0:T(8,128)S(1)}, f32[2,2,1024,256]{3,2,1,0:T(8,128)}, u32[]{:S(2)}) copy-start(f32[2,2,1024,256]{3,2,1,0:T(8,128)} %param.5) | copy-start | bytes 12582916
  132.5 3.2 %copy-start.2 = (f32[2,2,1024,256]{3,2,1,0:T(8,128)S(1)}, f32[2,2,1024,256]{3,2,1,0:T(8,128)}, u32[]{:S(2)}) copy-start(f32[2,2,1024,256]{3,2,1,0:T(8,128)} %param.5) | copy-start | bytes 12582916
  132.6 5.8 %copy-start.4 = (f32[256,1024]{1,0:T(8,128)S(1)}, f32[256,1024]{1,0:T(8,128)}, u32[]{:S(2)}) copy-start(f32[256,1024]{1,0:T(8,128)} %fusion.26) | copy-start | bytes 3145732
  132.6 5.8 %copy-start.5 = (f32[256,256]{1,0:T(8,128)S(1)}, f32[256,256]{1,0:T(8,128)}, u32[]{:S(2)}) copy-start(f32[256,256]{1,0:T(8,128)} %fusion.14) | copy-start | bytes 786436
  135.8 3.8 %copy-start.3 = (f32[256,1024]{1,0:T(8,128)S(1)}, f32[256,1024]{1,0:T(8,128)}, u32[]{:S(2)}) copy-start(f32[256,1024]{1,0:T(8,128)} %fusion.22) | copy-start | bytes 3145732
where the time goes:
time: 170 us; the launch traced here: 168 us
  blocking collectives  109 us (64%)
  matrix products  22.6 us (13%)
  starting transfers between devices  18.8 us (11%)
  local copies, waits for them, and re-layouts  12 us (7%)
  other arithmetic  3.78 us (2%)
  between operations  2.23 us (1%)
    all_gather x1, blocking collectives, shards(): gathered = lax.all_gather(spectra, 'rep', axis=1, tiled=True)  82 us
    unnamed x1, blocking collectives  26.9 us
    dot_general x17, matrix products, matmul(): jnp.dot(left, right, precision=lax.Precision.HIGHEST, preferred_element_t...  22.6 us
    all_to_all x1, starting transfers between devices, shards(): lax.all_to_all(gathered, 'tm', split_axis=3, concat_axis=0, tiled=True)  18.8 us
    unnamed x18, local copies, waits for them, and re-layouts  5.43 us
    slice x1, local copies, waits for them, and re-layouts, shards(): rep_im = replicas[1, column]  3.6 us
  transfers between devices with their start and end apart: 1, of which 0 were waited for; matrix products, arithmetic and copies ran while one was open for 6% of the time, Pallas kernels for 0%

commit v1 on v0

v1 whole, which is shorter than its diff:
```python
import functools
import math

import jax
import jax.numpy as jnp
from jax import lax
from jax.experimental import pallas as pl
from jax.experimental.pallas import tpu as pltpu
from jax.sharding import PartitionSpec as P

EPS = 1e-6
PLANES = 16
COLUMNS = 2
STEP = 2
ROWS = 256
MESH = pl.DeviceIdType.MESH
F32 = jnp.float32
BF16 = jnp.bfloat16


def split(value):
    high = value.astype(BF16)
    low = (value - high.astype(F32)).astype(BF16)
    return high, low


def lane_iota(shape):
    return lax.broadcasted_iota(jnp.int32, shape, len(shape) - 1)


def row_sums(value):
    folded = value[:, :128] + value[:, 128:]
    return jnp.sum(folded.T, axis=0, keepdims=True)


def fused(peers, bins_ref, snaps_hbm, reps_hbm, out_ref, snaps, reps, table, pieces, landed, blocks, left, right_hi,
          right_lo, norms, quads, shares, arrived, load_sem, piece_send, piece_recv, block_send, block_recv, share_send,
          share_recv):
    me = lax.axis_index("tm")
    spot = lax.axis_index("rep")
    column = spot // PLANES
    plane = spot % PLANES
    bin_count = bins_ref.shape[0]
    snap_rows, elem_rows, samples = snaps.shape
    grid_rows = reps.shape[2]
    elems = reps.shape[3]

    def rep_at(col, z):
        return col * PLANES + lax.rem(z + 2 * PLANES, PLANES)

    up = min(STEP, PLANES // 2)
    down = min(STEP, PLANES // 2 - 1)
    near = sorted(set([d for d in range(1, up + 1)] + [-d for d in range(1, down + 1)]
                      + [-d for d in range(1, up + 1)] + [d for d in range(1, down + 1)]))

    barrier = pltpu.get_barrier_semaphore()

    def greet(off, carry):
        other = lax.rem(me + off, peers)
        pl.semaphore_signal(barrier, inc=1, device_id={"tm": other, "rep": rep_at(column, plane)}, device_id_type=MESH)
        pl.semaphore_signal(barrier, inc=1, device_id={"tm": other, "rep": rep_at(1 - column, plane)},
                            device_id_type=MESH)
        return carry

    lax.fori_loop(1, peers, greet, 0)
    pl.semaphore_signal(barrier, inc=1, device_id={"tm": me, "rep": rep_at(1 - column, plane)}, device_id_type=MESH)
    for d in near:
        pl.semaphore_signal(barrier, inc=1, device_id={"tm": me, "rep": rep_at(column, plane + d)},
                            device_id_type=MESH)
    greeted = 2 * (peers - 1) + 1 + len(near)

    snap_load = pltpu.make_async_copy(snaps_hbm, snaps, load_sem.at[0])
    snap_load.start()
    rep_loads = [pltpu.make_async_copy(reps_hbm.at[:, b], reps.at[:, b], load_sem.at[1 + b]) for b in range(2)]
    for load in rep_loads:
        load.start()

    lane = lane_iota((1, 128))
    chosen = jnp.zeros((1, 128), jnp.int32)
    for k in range(bin_count):
        chosen = jnp.where((lane & 63) // 2 == k, bins_ref[k], chosen)
    index = lax.broadcasted_iota(jnp.int32, (32, 128), 0)
    unit = 2.0 * math.pi / samples
    coarse = ((index * 32 * chosen) & (samples - 1)).astype(F32) * unit
    fine = ((index * chosen) & (samples - 1)).astype(F32) * unit
    cos_a, sin_a = jnp.cos(coarse), jnp.sin(coarse)
    cos_b, sin_b = jnp.cos(fine), jnp.sin(fine)
    real = (lane & 1) == 0
    with_cos = jnp.where(real, cos_b, -sin_b)
    with_sin = jnp.where(real, -sin_b, -cos_b)
    for a in range(samples // 32):
        rows = cos_a[a : a + 1] * with_cos + sin_a[a : a + 1] * with_sin
        high = rows.astype(BF16).astype(F32)
        table[32 * a : 32 * a + 32, :] = jnp.where(lane < 64, high, rows - high).astype(BF16)
    window = 0.5 - 0.5 * jnp.cos(lane_iota((1, samples)).astype(F32) * unit)

    quarter = me % 4
    wide = lane_iota((1, 4 * 128))
    owner = (wide // 128) * 4 + (((wide // 32) % 4 + 4 - quarter) & 3)
    key = owner * 4 + (wide // 8) % 4
    spread = (lax.broadcasted_iota(jnp.int32, (128, 512), 0) & 63 == key).astype(F32).astype(BF16)

    snap_load.wait()
    shaded = snaps[...].reshape(snap_rows * elem_rows, samples) * window
    high, low = split(shaded)
    spectra = jnp.dot(jnp.concatenate([high, low], axis=0), table[...], preferred_element_type=F32)
    high, low = split(spectra)
    placed = jnp.dot(jnp.concatenate([high, low], axis=0), spread, preferred_element_type=F32)
    slabs = jnp.sum(placed.reshape(4, snap_rows, elem_rows, 512), axis=0)
    merged = jnp.zeros((elem_rows, 512), F32)
    for s in range(snap_rows):
        merged = jnp.where((wide & 7) == s, slabs[s], merged)
    for tile in range(4):
        part = merged[:, 128 * tile : 128 * tile + 128]
        for d in range(4):
            pieces[4 * tile + d] = part if d == 0 else pltpu.roll(part, 128 - 32 * d, 1)
    landed[column, me] = pieces[me]

    pl.semaphore_wait(barrier, greeted)

    def piece_copy(other, source, col, col_from):
        return pltpu.make_async_remote_copy(
            src_ref=pieces.at[other], dst_ref=landed.at[col_from, source], send_sem=piece_send.at[col, other],
            recv_sem=piece_recv.at[col_from, source], device_id={"tm": other, "rep": rep_at(col, plane)},
            device_id_type=MESH)

    def send_pieces(off, carry):
        other = lax.rem(me + off, peers)
        piece_copy(other, me, column, column).start()
        piece_copy(other, me, 1 - column, column).start()
        return carry

    piece_copy(me, me, 1 - column, column).start()
    lax.fori_loop(1, peers, send_pieces, 0)

    for b in range(2):
        rep_loads[b].wait()

        def prepare(step, carry, b=b):
            at = pl.ds(pl.multiple_of(step * 128, 128), 128)
            re = reps[0, b, at, :]
            im = reps[1, b, at, :]
            re_hi, re_lo = split(re)
            im_hi, im_lo = split(im)
            left[b, at, 0:elems] = re_hi
            left[b, at, elems : 2 * elems] = im_hi
            left[b, at, 2 * elems : 3 * elems] = re_lo
            left[b, at, 3 * elems : 4 * elems] = im_lo
            norms[b, pl.ds(step, 1), :] = row_sums(re * re + im * im)
            return carry

        lax.fori_loop(0, grid_rows // 128, prepare, 0)

    def take_pieces(off, carry):
        other = lax.rem(me + off, peers)
        piece_copy(other, other, column, column).wait_recv()
        piece_copy(other, other, column, 1 - column).wait_recv()
        return carry

    piece_copy(me, me, column, 1 - column).wait_recv()
    lax.fori_loop(1, peers, take_pieces, 0)

    for col in range(COLUMNS):
        tiles = []
        for tile in range(4):
            got = landed[col, 4 * tile]
            for d in range(1, 4):
                got = jnp.where(lane // 32 == d, landed[col, 4 * tile + d], got)
            tiles.append(got)
        for pair in range(2):
            first, second = tiles[2 * pair], tiles[2 * pair + 1]
            blocks[plane, col, pair] = jnp.where(lane & 16 == 0, first, pltpu.roll(second, 16, 1))
            blocks[plane, col, 2 + pair] = jnp.where(lane & 16 == 0, pltpu.roll(first, 112, 1), second)

    started = []

    def block_copy(owner_plane, to, slot):
        return pltpu.make_async_remote_copy(
            src_ref=blocks.at[owner_plane], dst_ref=blocks.at[owner_plane], send_sem=block_send.at[slot],
            recv_sem=block_recv.at[owner_plane], device_id={"tm": me, "rep": rep_at(column, plane + to)},
            device_id_type=MESH)

    def plane_at(offset):
        return lax.rem(plane + offset + 2 * PLANES, PLANES)

    def pass_on(owner_plane, to):
        copy = block_copy(owner_plane, to, len(started))
        copy.start()
        started.append(copy)

    waited = set()

    def wait_block(offset):
        block_copy(plane_at(offset), 0, 0).wait_recv()
        waited.add(offset)

    top, bottom = PLANES // 2, PLANES // 2 - 1
    for reach in range(STEP, 0, -1):
        if reach <= top:
            pass_on(plane, reach)
        if reach <= bottom:
            pass_on(plane, -reach)
    hub = STEP
    while hub < top:
        wait_block(-hub)
        for reach in range(min(STEP, top - hub), 0, -1):
            pass_on(plane_at(-hub), reach)
        if hub < bottom:
            wait_block(hub)
            for reach in range(min(STEP, bottom - hub), 0, -1):
                pass_on(plane_at(hub), -reach)
        hub += STEP
    for distance in range(1, top + 1):
        for offset in (-distance, distance):
            if offset not in waited and (offset < 0 or distance <= bottom):
                wait_block(offset)

    real = (lane & 8) == 0
    traces = []
    for b in range(2):
        energy = jnp.zeros((8, 128), F32)
        for col in range(COLUMNS):
            for pair in range(2):
                value = blocks[:, col, 2 * b + pair].reshape(PLANES * elem_rows, 128)
                turned = jnp.where(real, pltpu.roll(value, 120, 1), -pltpu.roll(value, 8, 1))
                energy = energy + jnp.sum((value * value).reshape(PLANES, 8, 128), axis=0)
                for part, entry in ((0, value), (1, turned)):
                    high, low = split(entry)
                    at = part * elems + col * PLANES * elem_rows
                    right_hi[b, at : at + PLANES * elem_rows, 128 * pair : 128 * pair + 128] = high
                    right_lo[b, at : at + PLANES * elem_rows, 128 * pair : 128 * pair + 128] = low
        traces.append(jnp.sum(energy))

    def project(step, carry):
        at = pl.ds(pl.multiple_of(step * ROWS, ROWS), ROWS)
        for b in range(2):
            proj = jnp.dot(left[b, at, : 2 * elems], right_hi[b], preferred_element_type=F32)
            proj += jnp.dot(left[b, at, : 2 * elems], right_lo[b], preferred_element_type=F32)
            proj += jnp.dot(left[b, at, 2 * elems :], right_hi[b], preferred_element_type=F32)
            square = proj * proj
            for piece in range(ROWS // 128):
                quads[b, pl.ds(step * (ROWS // 128) + piece, 1), :] = row_sums(square[128 * piece : 128 * piece + 128])
        return carry

    lax.fori_loop(0, grid_rows // ROWS, project, 0)

    snap_total = snap_rows * peers
    power = jnp.zeros((grid_rows // 128, 128), F32)
    for b in range(2):
        trace = traces[b] / snap_total + EPS
        power = power + quads[b] / snap_total / ((norms[b] + EPS) * trace / elems)
    power = power / bin_count
    for r in range(grid_rows // 128):
        shares[r] = power[r : r + 1]
    arrived[me] = shares[me // 2]

    def share_copy(other, source):
        return pltpu.make_async_remote_copy(
            src_ref=shares.at[other // 2], dst_ref=arrived.at[source], send_sem=share_send.at[other],
            recv_sem=share_recv.at[source], device_id={"tm": other, "rep": rep_at(column, plane)},
            device_id_type=MESH)

    def send_share(off, carry):
        share_copy(lax.rem(me + off, peers), me).start()
        return carry

    lax.fori_loop(1, peers, send_share, 0)

    def drain(off, carry):
        other = lax.rem(me + off, peers)
        piece_copy(other, me, column, column).wait_send()
        piece_copy(other, me, 1 - column, column).wait_send()
        share_copy(other, me).wait_send()
        return carry

    piece_copy(me, me, 1 - column, column).wait_send()
    lax.fori_loop(1, peers, drain, 0)
    for copy in started:
        copy.wait_send()

    def take_share(off, carry):
        other = lax.rem(me + off, peers)
        share_copy(other, other).wait_recv()
        return carry

    lax.fori_loop(1, peers, take_share, 0)
    total = jnp.sum(arrived[...], axis=0)
    odd = (me & 1) == 1
    out_ref[...] = jnp.where(odd, total[:, 64:], total[:, :64])


def shards(peers, snapshots, freq_bins, replicas):
    snap_rows, elem_rows, samples = snapshots.shape
    bins, grid_rows, elems = replicas.shape[1:]
    any_space = pl.BlockSpec(memory_space=pl.ANY)
    moves = 2 * PLANES
    out = pl.pallas_call(
        functools.partial(fused, peers),
        out_shape=jax.ShapeDtypeStruct((1, grid_rows // peers), F32),
        in_specs=[pl.BlockSpec(memory_space=pltpu.SMEM), any_space, any_space],
        out_specs=pl.BlockSpec(memory_space=pltpu.VMEM),
        scratch_shapes=[
            pltpu.VMEM(snapshots.shape, F32),
            pltpu.VMEM(replicas.shape, F32),
            pltpu.VMEM((samples, 128), BF16),
            pltpu.VMEM((peers, 8, 128), F32),
            pltpu.VMEM((COLUMNS, peers, 8, 128), F32),
            pltpu.VMEM((PLANES, COLUMNS, 4, 8, 128), F32),
            pltpu.VMEM((bins, grid_rows, 4 * elems), BF16),
            pltpu.VMEM((bins, 2 * elems, 256), BF16),
            pltpu.VMEM((bins, 2 * elems, 256), BF16),
            pltpu.VMEM((bins, grid_rows // 128, 128), F32),
            pltpu.VMEM((bins, grid_rows // 128, 128), F32),
            pltpu.VMEM((grid_rows // 128, 1, 128), F32),
            pltpu.VMEM((peers, 1, 128), F32),
            pltpu.SemaphoreType.DMA((3,)),
            pltpu.SemaphoreType.DMA((COLUMNS, peers)),
            pltpu.SemaphoreType.DMA((COLUMNS, peers)),
            pltpu.SemaphoreType.DMA((moves,)),
            pltpu.SemaphoreType.DMA((PLANES,)),
            pltpu.SemaphoreType.DMA((peers,)),
            pltpu.SemaphoreType.DMA((peers,)),
        ],
        compiler_params=pltpu.CompilerParams(collective_id=0, has_side_effects=True, vmem_limit_bytes=60 << 20),
    )(freq_bins, snapshots, replicas)
    return out.reshape(-1)


def solution(mesh):
    in_specs = (P("tm", "rep", None), P(), P(None, "tm", "rep", None))
    out_specs = P(("rep", "tm"))
    body = functools.partial(shards, mesh.shape["tm"])
    return jax.shard_map(body, mesh=mesh, in_specs=in_specs, out_specs=out_specs, check_vma=False)
```

time: 170 us -> 48.3 us (0.28)
  blocking collectives: 109 us -> 0 us
  Pallas kernels: 0 us -> 47 us
  matrix products: 22.6 us -> 0 us
  starting transfers between devices: 18.8 us -> 0 us
  local copies, waits for them, and re-layouts: 12 us -> 1.19 us
  other arithmetic: 3.78 us -> 0 us
  between operations: 2.23 us -> 0.01 us
    all_gather x1 -> x0, blocking collectives: 82 us -> none  [shards(): gathered = lax.all_gather(spectra, 'rep', axis=1, tiled=True)]
    pallas_call x0 -> x1, Pallas kernels: none -> 47 us  [shards(): pl.pallas_call(functools.partial(fused, peers), out_shape=jax.ShapeDtypeS...]
    unnamed x1 -> x0, blocking collectives: 26.9 us -> none
    dot_general x17 -> x0, matrix products: 22.6 us -> none  [matmul(): jnp.dot(left, right, precision=lax.Precision.HIGHEST, preferred_element_t...]
    all_to_all x1 -> x0, starting transfers between devices: 18.8 us -> none  [shards(): lax.all_to_all(gathered, 'tm', split_axis=3, concat_axis=0, tiled=True)]
    unnamed x18 -> x1, local copies, waits for them, and re-layouts: 5.43 us -> 1.19 us
    slice x1 -> x0, local copies, waits for them, and re-layouts: 3.6 us -> none  [shards(): rep_im = replicas[1, column]]
    reduce_sum x2 -> x0, other arithmetic: 2.43 us -> none  [the longest x1 1.71 us: shards(): norm_sq = jnp.sum(rep_re * rep_re + rep_im * rep_im, axis=1) + epsilon]
  transfers between devices with their start and end apart: 1 -> 0, of which waited for: 0 -> 0; matrix products, arithmetic and copies ran while one was open for 6% -> 0% of each run, Pallas kernels for 0% -> 0%
where the time goes in v1:
time: 48.3 us; the launch traced here: 48.2 us
  Pallas kernels  47 us (97%)
  local copies, waits for them, and re-layouts  1.19 us (2%)
    pallas_call x1, Pallas kernels, shards(): pl.pallas_call(functools.partial(fused, peers), out_shape=jax.ShapeDtypeS...  47 us
    unnamed x1, local copies, waits for them, and re-layouts  1.19 us

profile of v1, /device:TPU:1, one launch (start us, length us, event | category | flops | bytes accessed | tf_op | source)
XLA Modules:
  0.0 48.2 jit_solution(16881019462291719738)
XLA Ops:
  0.0 47.0 %shard_map.37 = f32[1,64]{1,0:T(1,128)} custom-call(s32[32]{0:T(128)} %bins_ref.1, f32[8,8,1024]{2,1,0:T(8,128)} %snaps_hbm.1, f32[2,2,1024,256]{3,2,1,0:T(8,128)} %reps_hbm.1), custom_call_target="tpu_custom_call" | custom-call | tf_op jit(solution)/shard_map/pallas_call | solution.py:297
  47.0 1.2 %copy.5 = f32[64]{0:T(128)} copy(f32[64]{0:T(128)} %bitcast.1) | data formatting | bytes 512

commit v2 on v1

v2 whole, which is shorter than its diff:
```python
import functools
import math

import jax
import jax.numpy as jnp
from jax import lax
from jax.experimental import pallas as pl
from jax.experimental.pallas import tpu as pltpu
from jax.sharding import PartitionSpec as P

EPS = 1e-6
PLANES = 16
COLUMNS = 2
UP = {6: (2, 1, -1), 2: (2, 1, -1)}
DOWN = {5: (2, 1, -1), 2: (1, -1)}
ROWS = 256
MESH = pl.DeviceIdType.MESH
F32 = jnp.float32
BF16 = jnp.bfloat16


def split(value):
    high = value.astype(BF16)
    low = (value - high.astype(F32)).astype(BF16)
    return high, low


def lane_iota(shape):
    return lax.broadcasted_iota(jnp.int32, shape, len(shape) - 1)


def row_sums(value):
    return jnp.sum(value.T, axis=0, keepdims=True)


def fused(peers, bins_hbm, snaps_hbm, reps_hbm, out_ref, bins_ref, snaps, reps, table, pieces, landed, blocks, left_hi, left_lo, halves, right_hi,
          right_lo, norms, quads, shares, arrived, load_sem, piece_send, piece_recv, block_send, block_recv, share_send,
          share_recv, ready, cross_send, cross_recv):
    me = lax.axis_index("tm")
    spot = lax.axis_index("rep")
    column = spot // PLANES
    plane = spot % PLANES
    bin_count = bins_ref.shape[0]
    snap_rows, elem_rows, samples = snaps.shape
    grid_rows = reps.shape[2]
    elems = reps.shape[3]

    def rep_at(col, z):
        return col * PLANES + lax.rem(z + 2 * PLANES, PLANES)

    legs = set()
    for tree in (UP, DOWN):
        for hub, leaves in tree.items():
            legs |= {hub} | set(leaves)
    near = sorted(legs | {-d for d in legs})

    def plane_at(offset):
        return lax.rem(plane + offset + PLANES, PLANES)

    bins_load = pltpu.make_async_copy(bins_hbm, bins_ref, load_sem.at[3])
    bins_load.start()
    snap_load = pltpu.make_async_copy(snaps_hbm, snaps, load_sem.at[0])
    snap_load.start()
    rep_loads = [pltpu.make_async_copy(reps_hbm.at[:, b], reps.at[:, b], load_sem.at[1 + b]) for b in range(2)]
    for load in rep_loads:
        load.start()


    barrier = pltpu.get_barrier_semaphore()

    def greet(off, carry):
        other = lax.rem(me + off, peers)
        pl.semaphore_signal(barrier, inc=1, device_id={"tm": other, "rep": rep_at(column, plane)}, device_id_type=MESH)
        return carry

    lax.fori_loop(1, peers, greet, 0)
    pl.semaphore_signal(barrier, inc=1, device_id={"tm": me, "rep": rep_at(1 - column, plane)}, device_id_type=MESH)
    def rank(z):
        return jnp.where(z < PLANES // 2, z, 3 * PLANES // 2 - 1 - z)

    greeted = peers
    answers = 0
    for d in near:
        higher = rank(plane_at(d)) > rank(plane)

        @pl.when(higher)
        def _(d=d):
            pl.semaphore_signal(barrier, inc=1, device_id={"tm": me, "rep": rep_at(column, plane + d)},
                                device_id_type=MESH)

        greeted = greeted + jnp.where(higher, 0, 1)
        answers = answers + jnp.where(higher, 1, 0)

    lane = lane_iota((1, 128))
    bins_load.wait()
    chosen = jnp.zeros((1, 128), jnp.int32)
    for k in range(bin_count):
        chosen = jnp.where((lane & 63) // 2 == k, bins_ref[k], chosen)
    index = lax.broadcasted_iota(jnp.int32, (32, 128), 0)
    unit = 2.0 * math.pi / samples
    coarse = ((index * 32 * chosen) & (samples - 1)).astype(F32) * unit
    fine = ((index * chosen) & (samples - 1)).astype(F32) * unit
    cos_a, sin_a = jnp.cos(coarse), jnp.sin(coarse)
    cos_b, sin_b = jnp.cos(fine), jnp.sin(fine)
    real = (lane & 1) == 0
    with_cos = jnp.where(real, cos_b, -sin_b)
    with_sin = jnp.where(real, -sin_b, -cos_b)
    for a in range(samples // 32):
        rows = cos_a[a : a + 1] * with_cos + sin_a[a : a + 1] * with_sin
        high = rows.astype(BF16).astype(F32)
        table[32 * a : 32 * a + 32, :] = jnp.where(lane < 64, high, rows - high).astype(BF16)
    window = 0.5 - 0.5 * jnp.cos(lane_iota((1, samples)).astype(F32) * unit)

    quarter = me % 4
    wide = lane_iota((1, 4 * 128))
    owner = (wide // 128) * 4 + (((wide // 32) % 4 + 4 - quarter) & 3)
    key = owner * 4 + (wide // 8) % 4
    spread = (lax.broadcasted_iota(jnp.int32, (128, 512), 0) & 63 == key).astype(F32).astype(BF16)

    snap_load.wait()
    shaded = snaps[...].reshape(snap_rows * elem_rows, samples) * window
    high, low = split(shaded)
    spectra = jnp.dot(jnp.concatenate([high, low], axis=0), table[...], preferred_element_type=F32)
    high, low = split(spectra)
    placed = jnp.dot(jnp.concatenate([high, low], axis=0), spread, preferred_element_type=F32)
    slabs = jnp.sum(placed.reshape(4, snap_rows, elem_rows, 512), axis=0)
    merged = jnp.zeros((elem_rows, 512), F32)
    for s in range(snap_rows):
        merged = jnp.where((wide & 7) == s, slabs[s], merged)
    for tile in range(4):
        part = merged[:, 128 * tile : 128 * tile + 128]
        for d in range(4):
            pieces[4 * tile + d] = part if d == 0 else pltpu.roll(part, 128 - 32 * d, 1)
    landed[me] = pieces[me]

    pl.semaphore_wait(barrier, greeted)
    for d in near:
        @pl.when(rank(plane_at(d)) < rank(plane))
        def _(d=d):
            pl.semaphore_signal(ready, inc=1, device_id={"tm": me, "rep": rep_at(column, plane + d)},
                                device_id_type=MESH)

    def piece_copy(other, source):
        return pltpu.make_async_remote_copy(
            src_ref=pieces.at[other], dst_ref=landed.at[source], send_sem=piece_send,
            recv_sem=piece_recv, device_id={"tm": other, "rep": rep_at(column, plane)}, device_id_type=MESH)

    def send_piece(off, carry):
        piece_copy(lax.rem(me + off, peers), me).start()
        return carry

    lax.fori_loop(1, peers, send_piece, 0)

    near_lanes = pl.ds(pl.multiple_of(128 * column, 128), 128)
    far_lanes = pl.ds(pl.multiple_of(128 * (1 - column), 128), 128)
    for b in range(2):
        rep_loads[b].wait()

        def prepare(step, carry, b=b):
            at = pl.ds(pl.multiple_of(step * 128, 128), 128)
            energy = jnp.zeros((128, 128), F32)
            for part in range(2):
                for half, lanes in ((0, near_lanes), (1, far_lanes)):
                    value = reps[part, b, at, lanes]
                    high, low = split(value)
                    to = 256 * half + 128 * part
                    left_hi[b, at, to : to + 128] = high
                    left_lo[b, at, to : to + 128] = low
                    energy = energy + value * value
            norms[b, pl.ds(step, 1), :] = row_sums(energy)
            return carry

        lax.fori_loop(0, grid_rows // 128, prepare, 0)

    all_pieces = pltpu.make_async_remote_copy(
        src_ref=pieces.at[pl.ds(0, peers - 1)], dst_ref=landed.at[pl.ds(0, peers - 1)], send_sem=piece_send,
        recv_sem=piece_recv, device_id={"tm": lax.rem(me + 1, peers), "rep": spot}, device_id_type=MESH)
    all_pieces.wait_recv()

    tiles = []
    for tile in range(4):
        got = landed[4 * tile]
        for d in range(1, 4):
            got = jnp.where(lane // 32 == d, landed[4 * tile + d], got)
        tiles.append(got)
    for pair in range(2):
        first, second = tiles[2 * pair], tiles[2 * pair + 1]
        blocks[0, plane, pair] = jnp.where(lane & 16 == 0, first, pltpu.roll(second, 16, 1))
        blocks[0, plane, 2 + pair] = jnp.where(lane & 16 == 0, pltpu.roll(first, 112, 1), second)

    def block_copy(offset, to):
        owner_plane = plane_at(offset)
        return pltpu.make_async_remote_copy(
            src_ref=blocks.at[0, owner_plane], dst_ref=blocks.at[0, owner_plane], send_sem=block_send,
            recv_sem=block_recv.at[owner_plane], device_id={"tm": me, "rep": rep_at(column, plane + to)},
            device_id_type=MESH)

    def cross(offset):
        owner_plane = plane_at(offset)
        pltpu.make_async_remote_copy(
            src_ref=blocks.at[0, owner_plane], dst_ref=blocks.at[1, owner_plane], send_sem=cross_send,
            recv_sem=cross_recv, device_id={"tm": me, "rep": rep_at(1 - column, plane)}, device_id_type=MESH).start()

    sent = []

    def pass_on(offset, to):
        block_copy(offset, to).start()
        sent.append((offset, to))

    def take(offset):
        block_copy(offset, 1).wait_recv()

    turned_sign = (lane & 8) == 0
    energies = [jnp.zeros((8, 128), F32) for _ in range(2)]

    def build(half):
        count = PLANES * elem_rows
        for b in range(2):
            for pair in range(2):
                value = blocks[half, :, 2 * b + pair].reshape(count, 128)
                turned = jnp.where(turned_sign, pltpu.roll(value, 120, 1), -pltpu.roll(value, 8, 1))
                energies[b] = energies[b] + jnp.sum((value * value).reshape(count // 8, 8, 128), axis=0)
                for part, entry in ((0, value), (1, turned)):
                    high, low = split(entry)
                    at = 256 * half + 128 * part
                    right_hi[b, at : at + 128, 128 * pair : 128 * pair + 128] = high
                    right_lo[b, at : at + 128, 128 * pair : 128 * pair + 128] = low

    def product(b, at, half):
        k = slice(256 * half, 256 * half + 256)
        value = jnp.dot(left_hi[b, at, k], right_hi[b, k, :], preferred_element_type=F32)
        value += jnp.dot(left_hi[b, at, k], right_lo[b, k, :], preferred_element_type=F32)
        return value + jnp.dot(left_lo[b, at, k], right_hi[b, k, :], preferred_element_type=F32)

    cross(0)

    @pl.when(answers > 0)
    def _():
        pl.semaphore_wait(ready, answers)

    for hub in sorted(UP, reverse=True):
        pass_on(0, hub)
    for hub in sorted(DOWN, reverse=True):
        pass_on(0, -hub)
    hubs = sorted([(hub, -hub, 1, leaves) for hub, leaves in UP.items()]
                  + [(hub, hub, -1, leaves) for hub, leaves in DOWN.items()])
    rest = []
    for hub, offset, way, leaves in hubs:
        take(offset)
        for leaf in leaves:
            pass_on(offset, way * leaf)
        cross(offset)
        rest += [(hub + leaf, -way * (hub + leaf)) for leaf in leaves]
    for _, offset in sorted(rest):
        take(offset)
        cross(offset)
    assert len(rest) + len(hubs) == PLANES - 1
    build(0)

    def project_near(step, carry):
        at = pl.ds(pl.multiple_of(step * ROWS, ROWS), ROWS)
        for b in range(2):
            halves[b, at, :] = product(b, at, 0)
        return carry

    lax.fori_loop(0, grid_rows // ROWS, project_near, 0)
    all_crossed = pltpu.make_async_remote_copy(
        src_ref=blocks.at[0], dst_ref=blocks.at[1], send_sem=cross_send, recv_sem=cross_recv,
        device_id={"tm": me, "rep": rep_at(1 - column, plane)}, device_id_type=MESH)
    all_crossed.wait_recv()
    build(1)

    def project(step, carry):
        at = pl.ds(pl.multiple_of(step * ROWS, ROWS), ROWS)
        for b in range(2):
            proj = halves[b, at, :] + product(b, at, 1)
            square = proj * proj
            square = square[:, :128] + square[:, 128:]
            for piece in range(ROWS // 128):
                quads[b, pl.ds(step * (ROWS // 128) + piece, 1), :] = row_sums(square[128 * piece : 128 * piece + 128])
        return carry

    lax.fori_loop(0, grid_rows // ROWS, project, 0)
    traces = [jnp.sum(energy) for energy in energies]

    snap_total = snap_rows * peers
    power = jnp.zeros((grid_rows // 128, 128), F32)
    for b in range(2):
        trace = traces[b] / snap_total + EPS
        power = power + quads[b] / snap_total / ((norms[b] + EPS) * trace / elems)
    power = power / bin_count
    for r in range(grid_rows // 128):
        shares[r] = power[r : r + 1]
    arrived[me] = shares[me // 2]

    def send_share(off, carry):
        other = lax.rem(me + off, peers)
        pltpu.make_async_remote_copy(
            src_ref=shares.at[other // 2], dst_ref=arrived.at[me], send_sem=share_send, recv_sem=share_recv,
            device_id={"tm": other, "rep": spot}, device_id_type=MESH).start()
        return carry

    lax.fori_loop(1, peers, send_share, 0)
    all_pieces.wait_send()
    all_crossed.wait_send()
    pltpu.make_async_remote_copy(
        src_ref=blocks.at[0, pl.ds(0, PLANES - 1)], dst_ref=blocks.at[0, pl.ds(0, PLANES - 1)], send_sem=block_send,
        recv_sem=block_recv.at[plane], device_id={"tm": me, "rep": rep_at(column, plane + 1)},
        device_id_type=MESH).wait_send()
    assert len(sent) == PLANES - 1
    all_shares = pltpu.make_async_remote_copy(
        src_ref=arrived.at[pl.ds(0, peers - 1)], dst_ref=arrived.at[pl.ds(0, peers - 1)], send_sem=share_send,
        recv_sem=share_recv, device_id={"tm": lax.rem(me + 1, peers), "rep": spot}, device_id_type=MESH)
    all_shares.wait_send()
    all_shares.wait_recv()
    total = jnp.sum(arrived[...], axis=0)
    odd = (me & 1) == 1
    out_ref[...] = jnp.where(odd, total[:, 64:], total[:, :64])


def shards(peers, snapshots, freq_bins, replicas):
    snap_rows, elem_rows, samples = snapshots.shape
    bins, grid_rows, elems = replicas.shape[1:]
    any_space = pl.BlockSpec(memory_space=pltpu.HBM)
    out = pl.pallas_call(
        functools.partial(fused, peers),
        out_shape=pltpu.VMEM((1, grid_rows // peers), F32),
        in_specs=[any_space, any_space, any_space],
        out_specs=pl.BlockSpec(memory_space=pltpu.VMEM),
        scratch_shapes=[
            pltpu.SMEM(freq_bins.shape, jnp.int32),
            pltpu.VMEM(snapshots.shape, F32),
            pltpu.VMEM(replicas.shape, F32),
            pltpu.VMEM((samples, 128), BF16),
            pltpu.VMEM((peers, 8, 128), F32),
            pltpu.VMEM((peers, 8, 128), F32),
            pltpu.VMEM((COLUMNS, PLANES, 4, 8, 128), F32),
            pltpu.VMEM((bins, grid_rows, 2 * elems), BF16),
            pltpu.VMEM((bins, grid_rows, 2 * elems), BF16),
            pltpu.VMEM((bins, grid_rows, 256), F32),
            pltpu.VMEM((bins, 2 * elems, 256), BF16),
            pltpu.VMEM((bins, 2 * elems, 256), BF16),
            pltpu.VMEM((bins, grid_rows // 128, 128), F32),
            pltpu.VMEM((bins, grid_rows // 128, 128), F32),
            pltpu.VMEM((grid_rows // 128, 1, 128), F32),
            pltpu.VMEM((peers, 1, 128), F32),
            pltpu.SemaphoreType.DMA((4,)),
            pltpu.SemaphoreType.DMA,
            pltpu.SemaphoreType.DMA,
            pltpu.SemaphoreType.DMA,
            pltpu.SemaphoreType.DMA((PLANES,)),
            pltpu.SemaphoreType.DMA,
            pltpu.SemaphoreType.DMA,
            pltpu.SemaphoreType.REGULAR,
            pltpu.SemaphoreType.DMA,
            pltpu.SemaphoreType.DMA,
        ],
        compiler_params=pltpu.CompilerParams(collective_id=0, has_side_effects=True, vmem_limit_bytes=60 << 20),
    )(freq_bins, snapshots, replicas)
    return out.reshape(-1)


def solution(mesh):
    in_specs = (P("tm", "rep", None), P(), P(None, "tm", "rep", None))
    out_specs = P(("rep", "tm"))
    body = functools.partial(shards, mesh.shape["tm"])
    return jax.shard_map(body, mesh=mesh, in_specs=in_specs, out_specs=out_specs, check_vma=False)
```

time: 48.3 us -> 40.8 us (0.84)
  Pallas kernels: 47 us -> 40.2 us
  local copies, waits for them, and re-layouts: 1.19 us -> 0.51 us
    pallas_call x1, Pallas kernels: 47 us -> 40.2 us  [shards(): pl.pallas_call(functools.partial(fused, peers), out_shape=pltpu.VMEM((1,...]
    unnamed x1, local copies, waits for them, and re-layouts: 1.19 us -> 0.51 us
where the time goes in v2:
time: 40.8 us; the launch traced here: 40.7 us
  Pallas kernels  40.2 us (99%)
  local copies, waits for them, and re-layouts  0.51 us (1%)
    pallas_call x1, Pallas kernels, shards(): pl.pallas_call(functools.partial(fused, peers), out_shape=pltpu.VMEM((1,...  40.2 us

profile of v2, /device:TPU:1, one launch (start us, length us, event | category | flops | bytes accessed | tf_op | source)
XLA Modules:
  0.0 40.7 jit_solution(11795459026472883862)
XLA Ops:
  0.0 40.2 %shard_map.37 = f32[1,64]{1,0:T(1,128)S(1)} custom-call(s32[32]{0:T(128)} %bins_hbm.1, f32[8,8,1024]{2,1,0:T(8,128)} %snaps_hbm.1, f32[2,2,1024,256]{3,2,1,0:T(8,128)} %reps_hbm.1), custom_call_target="tpu_custom_call" | custom-call | tf_op jit(solution)/shard_map/pallas_call | solution.py:325
  40.2 0.5 %copy.5 = f32[64]{0:T(128)} copy(f32[64]{0:T(128)S(1)} %bitcast.1) | data formatting | bytes 512

commit v3 on v2

--- a/solution.py
+++ b/solution.py
@@ -13,7 +13,8 @@
 COLUMNS = 2
 UP = {6: (2, 1, -1), 2: (2, 1, -1)}
 DOWN = {5: (2, 1, -1), 2: (1, -1)}
-ROWS = 256
+LATE = 6
+ROWS = 1024
 MESH = pl.DeviceIdType.MESH
 F32 = jnp.float32
 BF16 = jnp.bfloat16
@@ -35,7 +36,8 @@
 
 def fused(peers, bins_hbm, snaps_hbm, reps_hbm, out_ref, bins_ref, snaps, reps, table, pieces, landed, blocks, left_hi, left_lo, halves, right_hi,
           right_lo, norms, quads, shares, arrived, load_sem, piece_send, piece_recv, block_send, block_recv, share_send,
-          share_recv, ready, cross_send, cross_recv):
+          share_recv, ready, cross_send, cross_recv, late_recv, late,
+          left_late, right_late, window, spread):
     me = lax.axis_index("tm")
     spot = lax.axis_index("rep")
     column = spot // PLANES
@@ -92,12 +94,22 @@
         answers = answers + jnp.where(higher, 1, 0)
 
     lane = lane_iota((1, 128))
+    unit = 2.0 * math.pi / samples
+    window[...] = 0.5 - 0.5 * jnp.cos(lane_iota((1, samples)).astype(F32) * unit)
+    wide = lane_iota((1, 4 * 128))
+    quarter = me % 4
+    owner = (wide // 128) * 4 + (((wide // 32) % 4 + 4 - quarter) & 3)
+    key = owner * 4 + (wide // 8) % 4
+    spread[...] = (lax.broadcasted_iota(jnp.int32, (128, 512), 0) & 63 == key).astype(F32).astype(BF16)
+
+    for k in range(4):
+        blocks[1, plane_at(LATE + k)] = jnp.zeros((4, 8, 128), F32)
+    right_late[:, 192:, :] = jnp.zeros((2, 64, 256), BF16)
     bins_load.wait()
     chosen = jnp.zeros((1, 128), jnp.int32)
     for k in range(bin_count):
         chosen = jnp.where((lane & 63) // 2 == k, bins_ref[k], chosen)
     index = lax.broadcasted_iota(jnp.int32, (32, 128), 0)
-    unit = 2.0 * math.pi / samples
     coarse = ((index * 32 * chosen) & (samples - 1)).astype(F32) * unit
     fine = ((index * chosen) & (samples - 1)).astype(F32) * unit
     cos_a, sin_a = jnp.cos(coarse), jnp.sin(coarse)
@@ -109,20 +121,13 @@
         rows = cos_a[a : a + 1] * with_cos + sin_a[a : a + 1] * with_sin
         high = rows.astype(BF16).astype(F32)
         table[32 * a : 32 * a + 32, :] = jnp.where(lane < 64, high, rows - high).astype(BF16)
-    window = 0.5 - 0.5 * jnp.cos(lane_iota((1, samples)).astype(F32) * unit)
-
-    quarter = me % 4
-    wide = lane_iota((1, 4 * 128))
-    owner = (wide // 128) * 4 + (((wide // 32) % 4 + 4 - quarter) & 3)
-    key = owner * 4 + (wide // 8) % 4
-    spread = (lax.broadcasted_iota(jnp.int32, (128, 512), 0) & 63 == key).astype(F32).astype(BF16)
 
     snap_load.wait()
-    shaded = snaps[...].reshape(snap_rows * elem_rows, samples) * window
+    shaded = snaps[...].reshape(snap_rows * elem_rows, samples) * window[...]
     high, low = split(shaded)
     spectra = jnp.dot(jnp.concatenate([high, low], axis=0), table[...], preferred_element_type=F32)
     high, low = split(spectra)
-    placed = jnp.dot(jnp.concatenate([high, low], axis=0), spread, preferred_element_type=F32)
+    placed = jnp.dot(jnp.concatenate([high, low], axis=0), spread[...], preferred_element_type=F32)
     slabs = jnp.sum(placed.reshape(4, snap_rows, elem_rows, 512), axis=0)
     merged = jnp.zeros((elem_rows, 512), F32)
     for s in range(snap_rows):
@@ -153,20 +158,29 @@
 
     near_lanes = pl.ds(pl.multiple_of(128 * column, 128), 128)
     far_lanes = pl.ds(pl.multiple_of(128 * (1 - column), 128), 128)
+    turn = (8 * (2 * PLANES - LATE - plane)) & 127
+    turn_im = (turn + 32) & 127
     for b in range(2):
         rep_loads[b].wait()
 
         def prepare(step, carry, b=b):
             at = pl.ds(pl.multiple_of(step * 128, 128), 128)
             energy = jnp.zeros((128, 128), F32)
-            for part in range(2):
-                for half, lanes in ((0, near_lanes), (1, far_lanes)):
+            parts = []
+            for half, lanes in ((0, near_lanes), (1, far_lanes)):
+                for part in range(2):
                     value = reps[part, b, at, lanes]
                     high, low = split(value)
                     to = 256 * half + 128 * part
                     left_hi[b, at, to : to + 128] = high
                     left_lo[b, at, to : to + 128] = low
                     energy = energy + value * value
+                    parts.append(value)
+            last = jnp.where(lane < 32, pltpu.roll(parts[2], turn, 1), pltpu.roll(parts[3], turn_im, 1))
+            last = jnp.where(lane < 64, last, pltpu.roll(last, 64, 1))
+            high, low = split(last)
+            left_late[b, at, 0:128] = high
+            left_late[b, at, 128:256] = low
             norms[b, pl.ds(step, 1), :] = row_sums(energy)
             return carry
 
@@ -195,11 +209,15 @@
             recv_sem=block_recv.at[owner_plane], device_id={"tm": me, "rep": rep_at(column, plane + to)},
             device_id_type=MESH)
 
+    late_count = late.shape[0]
+
     def cross(offset):
         owner_plane = plane_at(offset)
+        slot = (offset - LATE) % PLANES
+        target, sem = (late.at[slot], late_recv) if slot < late_count else (blocks.at[1, owner_plane], cross_recv)
         pltpu.make_async_remote_copy(
-            src_ref=blocks.at[0, owner_plane], dst_ref=blocks.at[1, owner_plane], send_sem=cross_send,
-            recv_sem=cross_recv, device_id={"tm": me, "rep": rep_at(1 - column, plane)}, device_id_type=MESH).start()
+            src_ref=blocks.at[0, owner_plane], dst_ref=target, send_sem=cross_send, recv_sem=sem,
+            device_id={"tm": me, "rep": rep_at(1 - column, plane)}, device_id_type=MESH).start()
 
     sent = []
 
@@ -213,18 +231,31 @@
     turned_sign = (lane & 8) == 0
     energies = [jnp.zeros((8, 128), F32) for _ in range(2)]
 
+    def halves_of(value, b):
+        turned = jnp.where(turned_sign, pltpu.roll(value, 120, 1), -pltpu.roll(value, 8, 1))
+        energies[b] = energies[b] + jnp.sum((value * value).reshape(-1, 8, 128), axis=0)
+        return split(value) + split(turned)
+
     def build(half):
-        count = PLANES * elem_rows
         for b in range(2):
             for pair in range(2):
-                value = blocks[half, :, 2 * b + pair].reshape(count, 128)
-                turned = jnp.where(turned_sign, pltpu.roll(value, 120, 1), -pltpu.roll(value, 8, 1))
-                energies[b] = energies[b] + jnp.sum((value * value).reshape(count // 8, 8, 128), axis=0)
-                for part, entry in ((0, value), (1, turned)):
-                    high, low = split(entry)
-                    at = 256 * half + 128 * part
-                    right_hi[b, at : at + 128, 128 * pair : 128 * pair + 128] = high
-                    right_lo[b, at : at + 128, 128 * pair : 128 * pair + 128] = low
+                to = slice(128 * pair, 128 * pair + 128)
+                high, low, turned_high, turned_low = halves_of(
+                    blocks[half, :, 2 * b + pair].reshape(PLANES * elem_rows, 128), b)
+                at = 256 * half
+                right_hi[b, at : at + 128, to] = high
+                right_lo[b, at : at + 128, to] = low
+                right_hi[b, at + 128 : at + 256, to] = turned_high
+                right_lo[b, at + 128 : at + 256, to] = turned_low
+
+    def build_late():
+        for b in range(2):
+            for pair in range(2):
+                to = slice(128 * pair, 128 * pair + 128)
+                high, low, turned_high, turned_low = halves_of(
+                    late[:, 2 * b + pair].reshape(late_count * elem_rows, 128), b)
+                for at, entry in enumerate((high, turned_high, low, turned_low, high, turned_high)):
+                    right_late[b, 32 * at : 32 * at + 32, to] = entry
 
     def product(b, at, half):
         k = slice(256 * half, 256 * half + 256)
@@ -267,13 +298,30 @@
     all_crossed = pltpu.make_async_remote_copy(
         src_ref=blocks.at[0], dst_ref=blocks.at[1], send_sem=cross_send, recv_sem=cross_recv,
         device_id={"tm": me, "rep": rep_at(1 - column, plane)}, device_id_type=MESH)
-    all_crossed.wait_recv()
+    early_crossed = pltpu.make_async_remote_copy(
+        src_ref=blocks.at[0, pl.ds(0, PLANES - late_count)], dst_ref=blocks.at[1, pl.ds(0, PLANES - late_count)],
+        send_sem=cross_send, recv_sem=cross_recv, device_id={"tm": me, "rep": rep_at(1 - column, plane)},
+        device_id_type=MESH)
+    late_crossed = pltpu.make_async_remote_copy(
+        src_ref=late, dst_ref=late, send_sem=cross_send, recv_sem=late_recv,
+        device_id={"tm": me, "rep": rep_at(1 - column, plane)}, device_id_type=MESH)
+    early_crossed.wait_recv()
     build(1)
+
+    def project_far(step, carry):
+        at = pl.ds(pl.multiple_of(step * ROWS, ROWS), ROWS)
+        for b in range(2):
+            halves[b, at, :] += product(b, at, 1)
+        return carry
+
+    lax.fori_loop(0, grid_rows // ROWS, project_far, 0)
+    late_crossed.wait_recv()
+    build_late()
 
     def project(step, carry):
         at = pl.ds(pl.multiple_of(step * ROWS, ROWS), ROWS)
         for b in range(2):
-            proj = halves[b, at, :] + product(b, at, 1)
+            proj = halves[b, at, :] + jnp.dot(left_late[b, at, :], right_late[b], preferred_element_type=F32)
             square = proj * proj
             square = square[:, :128] + square[:, 128:]
             for piece in range(ROWS // 128):
@@ -354,6 +402,12 @@
             pltpu.SemaphoreType.REGULAR,
             pltpu.SemaphoreType.DMA,
             pltpu.SemaphoreType.DMA,
+            pltpu.SemaphoreType.DMA,
+            pltpu.VMEM((4, 4, 8, 128), F32),
+            pltpu.VMEM((bins, grid_rows, 256), BF16),
+            pltpu.VMEM((bins, 256, 256), BF16),
+            pltpu.VMEM((1, samples), F32),
+            pltpu.VMEM((128, 512), BF16),
         ],
         compiler_params=pltpu.CompilerParams(collective_id=0, has_side_effects=True, vmem_limit_bytes=60 << 20),
     )(freq_bins, snapshots, replicas)

time: 40.8 us -> 39.3 us (0.963)
  Pallas kernels: 40.2 us -> 38.7 us
    pallas_call x1, Pallas kernels: 40.2 us -> 38.7 us  [shards(): pl.pallas_call(functools.partial(fused, peers), out_shape=pltpu.VMEM((1,...]
where the time goes in v3:
time: 39.3 us; the launch traced here: 39.2 us
  Pallas kernels  38.7 us (98%)
  local copies, waits for them, and re-layouts  0.51 us (1%)
    pallas_call x1, Pallas kernels, shards(): pl.pallas_call(functools.partial(fused, peers), out_shape=pltpu.VMEM((1,...  38.7 us

profile of v3, /device:TPU:1, one launch (start us, length us, event | category | flops | bytes accessed | tf_op | source)
XLA Modules:
  0.0 39.2 jit_solution(10524514125840984692)
XLA Ops:
  0.0 38.7 %shard_map.37 = f32[1,64]{1,0:T(1,128)S(1)} custom-call(s32[32]{0:T(128)} %bins_hbm.1, f32[8,8,1024]{2,1,0:T(8,128)} %snaps_hbm.1, f32[2,2,1024,256]{3,2,1,0:T(8,128)} %reps_hbm.1), custom_call_target="tpu_custom_call" | custom-call | tf_op jit(solution)/shard_map/pallas_call | solution.py:373
  38.7 0.5 %copy.5 = f32[64]{0:T(128)} copy(f32[64]{0:T(128)S(1)} %bitcast.1) | data formatting | bytes 512

commit v4 on v3

--- a/solution.py
+++ b/solution.py
@@ -54,7 +54,13 @@
     for tree in (UP, DOWN):
         for hub, leaves in tree.items():
             legs |= {hub} | set(leaves)
-    near = sorted(legs | {-d for d in legs})
+    near = [(d, 0) for d in sorted(legs | {-d for d in legs})]
+    diagonal = {leaf for tree in (UP, DOWN) for hub, leaves in tree.items() if hub > 0 for leaf in leaves}
+    near += [(d, 1) for d in sorted(diagonal | {-d for d in diagonal})]
+
+    def side(other):
+        return 1 - column if other else column
+
 
     def plane_at(offset):
         return lax.rem(plane + offset + PLANES, PLANES)
@@ -82,12 +88,12 @@
 
     greeted = peers
     answers = 0
-    for d in near:
+    for d, other in near:
         higher = rank(plane_at(d)) > rank(plane)
 
         @pl.when(higher)
-        def _(d=d):
-            pl.semaphore_signal(barrier, inc=1, device_id={"tm": me, "rep": rep_at(column, plane + d)},
+        def _(d=d, other=other):
+            pl.semaphore_signal(barrier, inc=1, device_id={"tm": me, "rep": rep_at(side(other), plane + d)},
                                 device_id_type=MESH)
 
         greeted = greeted + jnp.where(higher, 0, 1)
@@ -139,10 +145,10 @@
     landed[me] = pieces[me]
 
     pl.semaphore_wait(barrier, greeted)
-    for d in near:
+    for d, other in near:
         @pl.when(rank(plane_at(d)) < rank(plane))
-        def _(d=d):
-            pl.semaphore_signal(ready, inc=1, device_id={"tm": me, "rep": rep_at(column, plane + d)},
+        def _(d=d, other=other):
+            pl.semaphore_signal(ready, inc=1, device_id={"tm": me, "rep": rep_at(side(other), plane + d)},
                                 device_id_type=MESH)
 
     def piece_copy(other, source):
@@ -151,7 +157,7 @@
             recv_sem=piece_recv, device_id={"tm": other, "rep": rep_at(column, plane)}, device_id_type=MESH)
 
     def send_piece(off, carry):
-        piece_copy(lax.rem(me + off, peers), me).start()
+        piece_copy(lax.rem(me + 1 + lax.rem(off + 10, peers - 1), peers), me).start()
         return carry
 
     lax.fori_loop(1, peers, send_piece, 0)
@@ -211,14 +217,16 @@
 
     late_count = late.shape[0]
 
-    def cross(offset):
+    def cross(offset, to=0):
         owner_plane = plane_at(offset)
-        slot = (offset - LATE) % PLANES
+        slot = (offset - to - LATE) % PLANES
         target, sem = (late.at[slot], late_recv) if slot < late_count else (blocks.at[1, owner_plane], cross_recv)
         pltpu.make_async_remote_copy(
             src_ref=blocks.at[0, owner_plane], dst_ref=target, send_sem=cross_send, recv_sem=sem,
-            device_id={"tm": me, "rep": rep_at(1 - column, plane)}, device_id_type=MESH).start()
-
+            device_id={"tm": me, "rep": rep_at(1 - column, plane + to)}, device_id_type=MESH).start()
+        crossed.append((offset, to))
+
+    crossed = []
     sent = []
 
     def pass_on(offset, to):
@@ -280,11 +288,16 @@
         take(offset)
         for leaf in leaves:
             pass_on(offset, way * leaf)
+        if hub > 0:
+            for leaf in leaves:
+                cross(offset, way * leaf)
         cross(offset)
-        rest += [(hub + leaf, -way * (hub + leaf)) for leaf in leaves]
-    for _, offset in sorted(rest):
+        rest += [(hub + leaf, -way * (hub + leaf), hub > 0) for leaf in leaves]
+    for _, offset, done in sorted(rest):
         take(offset)
-        cross(offset)
+        if not done:
+            cross(offset)
+    assert len(crossed) == PLANES
     assert len(rest) + len(hubs) == PLANES - 1
     build(0)
 
@@ -342,7 +355,7 @@
     arrived[me] = shares[me // 2]
 
     def send_share(off, carry):
-        other = lax.rem(me + off, peers)
+        other = lax.rem(me + 1 + lax.rem(off + 10, peers - 1), peers)
         pltpu.make_async_remote_copy(
             src_ref=shares.at[other // 2], dst_ref=arrived.at[me], send_sem=share_send, recv_sem=share_recv,
             device_id={"tm": other, "rep": spot}, device_id_type=MESH).start()

time: 39.3 us -> 38 us (0.967)
  Pallas kernels: 38.7 us -> 37.3 us
    pallas_call x1, Pallas kernels: 38.7 us -> 37.3 us  [shards(): pl.pallas_call(functools.partial(fused, peers), out_shape=pltpu.VMEM((1,...]
where the time goes in v4:
time: 38 us; the launch traced here: 37.9 us
  Pallas kernels  37.3 us (98%)
  local copies, waits for them, and re-layouts  0.51 us (1%)
    pallas_call x1, Pallas kernels, shards(): pl.pallas_call(functools.partial(fused, peers), out_shape=pltpu.VMEM((1,...  37.3 us

profile of v4, /device:TPU:1, one launch (start us, length us, event | category | flops | bytes accessed | tf_op | source)
XLA Modules:
  0.0 37.9 jit_solution(1478637323604147892)
XLA Ops:
  0.0 37.3 %shard_map.37 = f32[1,64]{1,0:T(1,128)S(1)} custom-call(s32[32]{0:T(128)} %bins_hbm.1, f32[8,8,1024]{2,1,0:T(8,128)} %snaps_hbm.1, f32[2,2,1024,256]{3,2,1,0:T(8,128)} %reps_hbm.1), custom_call_target="tpu_custom_call" | custom-call | tf_op jit(solution)/shard_map/pallas_call | solution.py:386
  37.4 0.5 %copy.5 = f32[64]{0:T(128)} copy(f32[64]{0:T(128)S(1)} %bitcast.1) | data formatting | bytes 512

commit v5 on v4

--- a/solution.py
+++ b/solution.py
@@ -50,17 +50,8 @@
     def rep_at(col, z):
         return col * PLANES + lax.rem(z + 2 * PLANES, PLANES)
 
-    legs = set()
-    for tree in (UP, DOWN):
-        for hub, leaves in tree.items():
-            legs |= {hub} | set(leaves)
-    near = [(d, 0) for d in sorted(legs | {-d for d in legs})]
-    diagonal = {leaf for tree in (UP, DOWN) for hub, leaves in tree.items() if hub > 0 for leaf in leaves}
-    near += [(d, 1) for d in sorted(diagonal | {-d for d in diagonal})]
-
-    def side(other):
-        return 1 - column if other else column
-
+    assert max(max(UP), max(DOWN)) <= 6
+    near = (-2, 2, -1, 1)
 
     def plane_at(offset):
         return lax.rem(plane + offset + PLANES, PLANES)
@@ -76,28 +67,18 @@
 
     barrier = pltpu.get_barrier_semaphore()
 
+    pl.semaphore_signal(barrier, inc=1, device_id={"tm": me, "rep": rep_at(1 - column, plane)}, device_id_type=MESH)
+    for d in near:
+        pl.semaphore_signal(barrier, inc=1, device_id={"tm": me, "rep": rep_at(column, plane + d)},
+                            device_id_type=MESH)
+
     def greet(off, carry):
         other = lax.rem(me + off, peers)
         pl.semaphore_signal(barrier, inc=1, device_id={"tm": other, "rep": rep_at(column, plane)}, device_id_type=MESH)
         return carry
 
     lax.fori_loop(1, peers, greet, 0)
-    pl.semaphore_signal(barrier, inc=1, device_id={"tm": me, "rep": rep_at(1 - column, plane)}, device_id_type=MESH)
-    def rank(z):
-        return jnp.where(z < PLANES // 2, z, 3 * PLANES // 2 - 1 - z)
-
-    greeted = peers
-    answers = 0
-    for d, other in near:
-        higher = rank(plane_at(d)) > rank(plane)
-
-        @pl.when(higher)
-        def _(d=d, other=other):
-            pl.semaphore_signal(barrier, inc=1, device_id={"tm": me, "rep": rep_at(side(other), plane + d)},
-                                device_id_type=MESH)
-
-        greeted = greeted + jnp.where(higher, 0, 1)
-        answers = answers + jnp.where(higher, 1, 0)
+    greeted = peers + len(near)
 
     lane = lane_iota((1, 128))
     unit = 2.0 * math.pi / samples
@@ -145,11 +126,14 @@
     landed[me] = pieces[me]
 
     pl.semaphore_wait(barrier, greeted)
-    for d, other in near:
-        @pl.when(rank(plane_at(d)) < rank(plane))
-        def _(d=d, other=other):
-            pl.semaphore_signal(ready, inc=1, device_id={"tm": me, "rep": rep_at(side(other), plane + d)},
+
+    def report(sem):
+        for d in (-2, 2):
+            pl.semaphore_signal(sem, inc=1, device_id={"tm": me, "rep": rep_at(column, plane + d)},
                                 device_id_type=MESH)
+
+    report(ready.at[0])
+    pl.semaphore_signal(ready.at[0], inc=1, device_id={"tm": me, "rep": rep_at(1 - column, plane)}, device_id_type=MESH)
 
     def piece_copy(other, source):
         return pltpu.make_async_remote_copy(
@@ -166,7 +150,7 @@
     far_lanes = pl.ds(pl.multiple_of(128 * (1 - column), 128), 128)
     turn = (8 * (2 * PLANES - LATE - plane)) & 127
     turn_im = (turn + 32) & 127
-    for b in range(2):
+    def prepare_bin(b):
         rep_loads[b].wait()
 
         def prepare(step, carry, b=b):
@@ -192,6 +176,10 @@
 
         lax.fori_loop(0, grid_rows // 128, prepare, 0)
 
+    prepare_bin(0)
+
+    pl.semaphore_wait(ready.at[0], 3)
+    report(ready.at[1])
     all_pieces = pltpu.make_async_remote_copy(
         src_ref=pieces.at[pl.ds(0, peers - 1)], dst_ref=landed.at[pl.ds(0, peers - 1)], send_sem=piece_send,
         recv_sem=piece_recv, device_id={"tm": lax.rem(me + 1, peers), "rep": spot}, device_id_type=MESH)
@@ -273,14 +261,12 @@
 
     cross(0)
 
-    @pl.when(answers > 0)
-    def _():
-        pl.semaphore_wait(ready, answers)
-
+    pl.semaphore_wait(ready.at[1], 2)
     for hub in sorted(UP, reverse=True):
         pass_on(0, hub)
     for hub in sorted(DOWN, reverse=True):
         pass_on(0, -hub)
+    prepare_bin(1)
     hubs = sorted([(hub, -hub, 1, leaves) for hub, leaves in UP.items()]
                   + [(hub, hub, -1, leaves) for hub, leaves in DOWN.items()])
     rest = []
@@ -412,7 +398,7 @@
             pltpu.SemaphoreType.DMA((PLANES,)),
             pltpu.SemaphoreType.DMA,
             pltpu.SemaphoreType.DMA,
-            pltpu.SemaphoreType.REGULAR,
+            pltpu.SemaphoreType.REGULAR((2,)),
             pltpu.SemaphoreType.DMA,
             pltpu.SemaphoreType.DMA,
             pltpu.SemaphoreType.DMA,

time: 38 us -> 36.7 us (0.966)
  Pallas kernels: 37.3 us -> 36 us
    pallas_call x1, Pallas kernels: 37.3 us -> 36 us  [shards(): pl.pallas_call(functools.partial(fused, peers), out_shape=pltpu.VMEM((1,...]
where the time goes in v5:
time: 36.7 us; the launch traced here: 36.5 us
  Pallas kernels  36 us (98%)
  local copies, waits for them, and re-layouts  0.51 us (1%)
    pallas_call x1, Pallas kernels, shards(): pl.pallas_call(functools.partial(fused, peers), out_shape=pltpu.VMEM((1,...  36 us

profile of v5, /device:TPU:1, one launch (start us, length us, event | category | flops | bytes accessed | tf_op | source)
XLA Modules:
  0.0 36.5 jit_solution(6739623502083800380)
XLA Ops:
  0.0 36.0 %shard_map.37 = f32[1,64]{1,0:T(1,128)S(1)} custom-call(s32[32]{0:T(128)} %bins_hbm.1, f32[8,8,1024]{2,1,0:T(8,128)} %snaps_hbm.1, f32[2,2,1024,256]{3,2,1,0:T(8,128)} %reps_hbm.1), custom_call_target="tpu_custom_call" | custom-call | tf_op jit(solution)/shard_map/pallas_call | solution.py:372
  36.0 0.5 %copy.5 = f32[64]{0:T(128)} copy(f32[64]{0:T(128)S(1)} %bitcast.1) | data formatting | bytes 512

commit v6 on v5

--- a/solution.py
+++ b/solution.py
@@ -67,7 +67,11 @@
 
     barrier = pltpu.get_barrier_semaphore()
 
-    pl.semaphore_signal(barrier, inc=1, device_id={"tm": me, "rep": rep_at(1 - column, plane)}, device_id_type=MESH)
+    @pl.when(column == 0)
+    def _():
+        pl.semaphore_signal(barrier, inc=1, device_id={"tm": me, "rep": rep_at(1 - column, plane)},
+                            device_id_type=MESH)
+
     for d in near:
         pl.semaphore_signal(barrier, inc=1, device_id={"tm": me, "rep": rep_at(column, plane + d)},
                             device_id_type=MESH)
@@ -78,7 +82,7 @@
         return carry
 
     lax.fori_loop(1, peers, greet, 0)
-    greeted = peers + len(near)
+    greeted = peers - 1 + len(near) + column
 
     lane = lane_iota((1, 128))
     unit = 2.0 * math.pi / samples
@@ -132,8 +136,14 @@
             pl.semaphore_signal(sem, inc=1, device_id={"tm": me, "rep": rep_at(column, plane + d)},
                                 device_id_type=MESH)
 
+    def report_across(sem):
+        pl.semaphore_signal(sem, inc=1, device_id={"tm": me, "rep": rep_at(1 - column, plane)}, device_id_type=MESH)
+
     report(ready.at[0])
-    pl.semaphore_signal(ready.at[0], inc=1, device_id={"tm": me, "rep": rep_at(1 - column, plane)}, device_id_type=MESH)
+
+    @pl.when(column == 1)
+    def _():
+        report_across(ready.at[0])
 
     def piece_copy(other, source):
         return pltpu.make_async_remote_copy(
@@ -178,8 +188,13 @@
 
     prepare_bin(0)
 
-    pl.semaphore_wait(ready.at[0], 3)
+    pl.semaphore_wait(ready.at[0], 3 - column)
     report(ready.at[1])
+
+    @pl.when(column == 0)
+    def _():
+        report_across(ready.at[1])
+
     all_pieces = pltpu.make_async_remote_copy(
         src_ref=pieces.at[pl.ds(0, peers - 1)], dst_ref=landed.at[pl.ds(0, peers - 1)], send_sem=piece_send,
         recv_sem=piece_recv, device_id={"tm": lax.rem(me + 1, peers), "rep": spot}, device_id_type=MESH)
@@ -259,9 +274,9 @@
         value += jnp.dot(left_hi[b, at, k], right_lo[b, k, :], preferred_element_type=F32)
         return value + jnp.dot(left_lo[b, at, k], right_hi[b, k, :], preferred_element_type=F32)
 
+
+    pl.semaphore_wait(ready.at[1], 2 + column)
     cross(0)
-
-    pl.semaphore_wait(ready.at[1], 2)
     for hub in sorted(UP, reverse=True):
         pass_on(0, hub)
     for hub in sorted(DOWN, reverse=True):

time: 36.7 us -> 36.7 us (level)
  no operation moved by 1% of the time
where the time goes in v6:
time: 36.7 us; the launch traced here: 36.5 us
  Pallas kernels  36 us (98%)
  local copies, waits for them, and re-layouts  0.51 us (1%)
    pallas_call x1, Pallas kernels, shards(): pl.pallas_call(functools.partial(fused, peers), out_shape=pltpu.VMEM((1,...  36 us

profile of v6, /device:TPU:1, one launch (start us, length us, event | category | flops | bytes accessed | tf_op | source)
XLA Modules:
  0.0 36.5 jit_solution(5385486786377955223)
XLA Ops:
  0.0 36.0 %shard_map.37 = f32[1,64]{1,0:T(1,128)S(1)} custom-call(s32[32]{0:T(128)} %bins_hbm.1, f32[8,8,1024]{2,1,0:T(8,128)} %snaps_hbm.1, f32[2,2,1024,256]{3,2,1,0:T(8,128)} %reps_hbm.1), custom_call_target="tpu_custom_call" | custom-call | tf_op jit(solution)/shard_map/pallas_call | solution.py:387
  36.0 0.5 %copy.5 = f32[64]{0:T(128)} copy(f32[64]{0:T(128)S(1)} %bitcast.1) | data formatting | bytes 512
